TPU v7x, 128 devices: a whole 4x4x4 slice. The times are simulated.
128 devices in a mesh: dp: 16 (over z, y), expert: 8 (over x, core).
Axes of the slice: x: 4, y: 4, z: 4, core: 2. Of those that a mesh axis runs over, the one named last changes fastest.
Arguments:
- tokens: bfloat16 [2048, 4096], P('dp'), may hold values from -6 to 6
- expert_ids: int32 [2048, 2], P('dp'), may hold values from 0 to 7, all different within a row; in each aligned block of 128 rows (0 to 127, 128 to 255, ...) at most 96 rows name the same one
- gate_weights: float32 [2048, 2], P('dp'), may hold values from 0.2 to 1
- live_counts: int32 [16], P('dp'), may hold values from 64 to 128, as said below
- w_gate: bfloat16 [8, 4096, 8192], P('expert', None, 'dp'), may hold values from -0.09375 to 0.09375
- w_up: bfloat16 [8, 4096, 8192], P('expert', None, 'dp'), may hold values from -0.09375 to 0.09375
- w_down: bfloat16 [8, 8192, 4096], P('expert', 'dp'), may hold values from -0.0625 to 0.0625
Outputs:
- mixed: bfloat16 [2048, 4096], P('dp')
- total_loads: int32 [8], replicated
Inputs may be any that keep to these rules, and one draw needn't show every extreme that they name: `expert_ids`: each token names two different experts. Among the tokens of one rank no expert is named more than 96 times, a bound that some block reaches in some ranks. Rank r's first live_counts[r] tokens are live, the rest are padding. Some rank has all 128 tokens live.
All inputs are finite; a program needn't handle non-finite values.
Results may differ from a plain program's by a relative error of at most 0.017.
Values may be sent and summed in bfloat16 or wider, within the bound.
No kernel may reach another device: no remote copies, remote signals or barrier semaphores. Data moves between devices by JAX's collectives and lax.ppermute only.
A program may use at most 128 MiB of HBM per device.

v0:
```python
import jax
import jax.numpy as jnp
from jax import lax
from jax.sharding import Mesh
from jax.sharding import PartitionSpec as P

DP = ("dp_0", "dp_1")


def split_up(shard, dim, size):
    before, after = (shard.shape[:dim], shard.shape[dim + 1 :])
    return jnp.moveaxis(shard.reshape(*before, size, -1, *after), dim, 0)


def sum_at_owner(shard, axis, dim):
    size = lax.axis_size(axis)
    tiles = lax.all_to_all(split_up(shard, dim, size), axis, 0, 0, tiled=True)
    return jnp.sum(tiles.astype(jnp.float32), axis=0)


def from_everyone(shard, axis):
    copies = jnp.broadcast_to(shard, (lax.axis_size(axis), *shard.shape))
    return lax.all_to_all(copies, axis, split_axis=0, concat_axis=0, tiled=True)


def laid_out(tiles, dim):
    dims = list(tiles.shape[1:])
    dims[dim] *= tiles.shape[0]
    return jnp.moveaxis(tiles, 0, dim).reshape(dims)


def gather_directly(shard, axis, dim):
    tiles = from_everyone(shard, axis)
    return laid_out(tiles, dim)


def over_axes(shard, axes):
    for axis in axes:
        shard = lax.psum(shard, axis)
    return shard


def plan_routes(expert_ids, live_total, n_experts, capacity):
    row_count = expert_ids.shape[0]
    is_live = jnp.arange(row_count, dtype=jnp.int32) < live_total
    flat_ids = expert_ids.reshape(-1)
    live_pairs = jnp.repeat(is_live, 2)
    one_hot = (
        (flat_ids[:, None] == jnp.arange(n_experts, dtype=jnp.int32)[None, :]) & live_pairs[:, None]
    ).astype(jnp.int32)
    earlier = jnp.cumsum(one_hot, axis=0) - one_hot
    slot_index = jnp.sum(earlier * one_hot, axis=1)
    targets = jnp.where(live_pairs, flat_ids * capacity + slot_index, -1)
    return (targets.reshape(row_count, 2), jnp.sum(one_hot, axis=0))


def dispatch_rows(tokens, targets, slots_all):
    wanted = targets.reshape(-1)[None, :] == jnp.arange(slots_all, dtype=jnp.int32)[:, None]
    wanted = jnp.any(wanted.reshape(slots_all, -1, 2), axis=2).astype(jnp.bfloat16)
    return jnp.dot(wanted, tokens, preferred_element_type=jnp.float32).astype(jnp.bfloat16)


def per_device(tokens, expert_ids, gate_weights, live_counts, w_gate, w_up, w_down):
    n_experts = lax.axis_size("expert")
    my_expert = lax.axis_index("expert")
    capacity = 3 * tokens.shape[0] // 4
    targets, expert_loads = plan_routes(expert_ids, live_counts[0], n_experts, capacity)
    local_slots = targets - my_expert * capacity
    outbound = dispatch_rows(tokens, local_slots, capacity)
    gathered = lax.all_gather(outbound, DP, axis=0, tiled=True)
    gate_matrix = w_gate[0]
    up_matrix = w_up[0]
    down_matrix = w_down[0]
    gate_act = jnp.dot(gathered, gate_matrix, preferred_element_type=jnp.float32)
    up_act = jnp.dot(gathered, up_matrix, preferred_element_type=jnp.float32)
    hidden = (jax.nn.silu(gate_act) * up_act).astype(jnp.bfloat16)
    summed = lax.psum_scatter(
        jnp.dot(hidden, down_matrix, preferred_element_type=jnp.float32).astype(jnp.bfloat16),
        DP,
        scatter_dimension=0,
        tiled=True,
    )
    is_mine = (local_slots >= 0) & (local_slots < capacity)
    pick_index = jnp.where(is_mine, local_slots, 0)
    selected = summed[pick_index].astype(jnp.float32)
    weights = jnp.where(is_mine, gate_weights, jnp.zeros_like(gate_weights))
    weighted = jnp.sum(weights[:, :, None] * selected, axis=1)
    share = sum_at_owner(weighted.astype(jnp.bfloat16), "expert", 0).astype(jnp.bfloat16)
    mixed = gather_directly(share, "expert", 0)
    total_loads = over_axes(expert_loads, DP)
    return (mixed, total_loads)


def solution(mesh):
    torus = Mesh(mesh.devices.reshape(4, 4, mesh.shape["expert"]), ("dp_0", "dp_1", "expert"))
    in_specs = (
        P(DP, None),
        P(DP, None),
        P(DP, None),
        P(DP),
        P("expert", None, DP),
        P("expert", None, DP),
        P("expert", DP, None),
    )
    out_specs = (P(DP, None), P())
    return jax.shard_map(
        per_device, mesh=torus, in_specs=in_specs, out_specs=out_specs, check_vma=False
    )
```

profile of v0, /device:TPU:2, one launch (start us, length us, event | category | flops | bytes accessed | tf_op | source)
XLA Modules:
  0.0 302.2 jit_solution(7526284278638504880)
XLA Ops:
  7.2 0.8 broadcast_multiply_fusion
  8.0 0.8 copy.17
  9.8 0.1 broadcast_in_dim.27
  10.1 0.1 and.20
  10.3 0.6 reduce-window.6
  10.9 0.2 slice_reduce_fusion
  11.2 0.1 convert_reduce_fusion
  11.3 0.1 reduce_sum.42
  11.5 0.8 copy.20
  12.5 1.2 convolution_convert_fusion.1
  13.8 92.4 %all-gather.2.cloned.1.call-done = bf16[1536,4096]{1,0:T(8,128)(2,1)} async-done(((bf16[96,4096]{1,0:T(8,128)(2,1)}), bf16[1536,4096]{1,0:T(8,128)(2,1)}) %all-gather.2.cloned.1.call-update) | async-done | bytes 12582928 | tf_op jit(solution)/shard_map/all_gather | solution.py:70
  106.2 12.0 %fusion.3 = f32[1536,512]{1,0:T(8,128)} fusion(bf16[1536,4096]{1,0:T(8,128)(2,1)} %all-gather.2.cloned.1.call-done, bf16[1,4096,512]{2,1,0:T(8,128)(2,1)} %param.11), kind=kOutput, calls=%fused_computation.6 | convolution fusion | flops 6442450944 | bytes 19922944 | tf_op jit(solution)/shard_map/dot_general | solution.py:74
  118.2 21.8 %convolution_convert_fusion = bf16[1536,4096]{1,0:T(8,128)(2,1)} fusion(bf16[1,512,4096]{2,1,0:T(8,128)(2,1)} %param.13, bf16[1536,4096]{1,0:T(8,128)(2,1)} %all-gather.2.cloned.1.call-done, bf16[1,4096,512]{2,1,0:T(8,128)(2,1)} %param.12, f32[1536,512]{1,0:T(8,128)} %fusion.3), kind=kOutput, calls=%fused_computation.1 | convolution fusion | flops 12895911936 | bytes 36700160 | tf_op jit(solution)/shard_map/dot_general | solution.py:78
  140.2 95.1 %reduce-scatter.2.cloned.1.call-done = bf16[96,4096]{1,0:T(8,128)(2,1)} async-done(((bf16[1536,4096]{1,0:T(8,128)(2,1)}), bf16[96,4096]{1,0:T(8,128)(2,1)}) %reduce-scatter.2.cloned.1.call-update) | async-done | bytes 786448 | tf_op jit(solution)/shard_map/reduce_scatter | solution.py:77
  235.3 5.1 %gather_fusion = bf16[256,4096]{1,0:T(8,128)(2,1)S(1)} fusion(bf16[96,4096]{1,0:T(8,128)(2,1)} %reduce-scatter.2.cloned.1.call-done, s32[1024]{0:T(1024)S(1)} %pad_clamp_fusion), kind=kCustom, calls=%fused_computation | custom fusion | bytes 4195328 | tf_op jit(solution)/shard_map/gather | solution.py:85
  240.4 4.0 %reshape.63 = f32[128,2,4096]{2,1,0:T(2,128)} reshape(bf16[256,4096]{1,0:T(8,128)(2,1)S(1)} %gather_fusion) | data formatting | bytes 6291456 | tf_op jit(solution)/shard_map/convert_element_type | solution.py:85
  244.4 8.7 %multiply_reduce_fusion = bf16[128,4096]{1,0:T(8,128)(2,1)S(1)} fusion(f32[128,2,4096]{2,1,0:T(2,128)} %reshape.63, f32[128,2]{1,0:T(8,128)S(1)} %get-tuple-element.4), kind=kLoop, calls=%fused_computation.8 | loop fusion | flops 1572864 | bytes 5243904 | tf_op jit(solution)/shard_map/reduce_sum | solution.py:87
  253.1 19.2 %all_to_all.10 = bf16[8,16,4096]{2,1,0:T(8,128)(2,1)S(1)} all-to-all(bf16[8,16,4096]{2,1,0:T(8,128)(2,1)S(1)} %bitcast.29), channel_id=1, replica_groups=mesh['dp_0'=4,'dp_1'=4,'expert'=8] {'expert'}, dimensions={0} | all-to-all | bytes 2097152 | tf_op jit(solution)/shard_map/all_to_all | solution.py:17
  272.3 0.1 reduce_sum.44
  272.4 1.1 broadcast_in_dim.31
  273.5 4.9 %all-to-all-start.1 = ((bf16[8,16,4096]{2,1,0:T(8,128)(2,1)}), bf16[8,16,4096]{2,1,0:T(8,128)(2,1)S(1)}, u32[]{:S(2)}, u32[]{:S(2)}) async-start(bf16[8,16,4096]{2,1,0:T(8,128)(2,1)} %broadcast_in_dim.31), calls=%async_computation.2 | async-start | bytes 2097152 | tf_op jit(solution)/shard_map/all_to_all | solution.py:23
  278.4 8.2 %psum.14 = s32[8]{0:T(128)S(1)} all-reduce(s32[8]{0:T(128)S(1)} %get-tuple-element.2), channel_id=1, replica_groups=mesh['dp_0'=4,'dp_1'=4,'expert'=8] {'dp_0'}, use_global_device_ids=true, to_apply=%region_8.9 | all-reduce | flops 8 | bytes 64 | tf_op jit(solution)/shard_map/psum | solution.py:39
  286.5 7.8 %psum.15 = s32[8]{0:T(128)} all-reduce(s32[8]{0:T(128)S(1)} %psum.14), channel_id=1, replica_groups=mesh['dp_0'=4,'dp_1'=4,'expert'=8] {'dp_1'}, use_global_device_ids=true, to_apply=%region_9.10 | all-reduce | flops 8 | bytes 64 | tf_op jit(solution)/shard_map/psum | solution.py:39
  294.4 1.0 copy.25
  (23 shorter events, 1.1 us)
Async XLA Ops:
  7.2 5.3 %copy-start = (bf16[128,4096]{1,0:T(8,128)(2,1)S(1)}, bf16[128,4096]{1,0:T(8,128)(2,1)}, u32[]{:S(2)}) copy-start(bf16[128,4096]{1,0:T(8,128)(2,1)} %param.7) | copy-start | bytes 3145732
  7.2 99.0 %all-gather.2.cloned.1.call-start = ((), (), s32[]{:S(2)}) async-start(), calls=%async_computation.3 | async-start | bytes 13369344 | tf_op jit(solution)/shard_map/all_gather | solution.py:70
  13.8 221.5 %reduce-scatter.2.cloned.1.call-start = ((), (), s32[]{:S(2)}) async-start(), calls=%async_computation.4 | async-start | bytes 13369344 | tf_op jit(solution)/shard_map/reduce_scatter | solution.py:77
  273.5 20.9 %all-to-all-start.1 = ((bf16[8,16,4096]{2,1,0:T(8,128)(2,1)}), bf16[8,16,4096]{2,1,0:T(8,128)(2,1)S(1)}, u32[]{:S(2)}, u32[]{:S(2)}) async-start(bf16[8,16,4096]{2,1,0:T(8,128)(2,1)} %broadcast_in_dim.31), calls=%async_computation.2 | async-start | bytes 2097152 | tf_op jit(solution)/shard_map/all_to_all | solution.py:23
Sparse Core Ops, SparseCore 0:
  13.9 92.2 all-gather.1
  140.1 95.1 reduce-scatter.1
where the time goes:
time: 303 us; the launch traced here: 302 us
  waiting for transfers between devices  188 us (62%)
  blocking collectives  35.2 us (12%)
  matrix products  35.1 us (12%)
  between operations  14.8 us (5%)
  local copies, waits for them, and re-layouts  14.1 us (5%)
  other arithmetic  10.5 us (3%)
  starting transfers between devices  4.93 us (2%)
    reduce_scatter x1, waiting for transfers between devices, per_device(): lax.psum_scatter(jnp.dot(hidden, down_matrix, preferred_element_type=jnp....  95.1 us
    all_gather x1, waiting for transfers between devices, per_device(): gathered = lax.all_gather(outbound, DP, axis=0, tiled=True)  92.4 us
    dot_general x1, matrix products, per_device(): jnp.dot(hidden, down_matrix, preferred_element_type=jnp.float32)  21.8 us
    all_to_all x1, blocking collectives, sum_at_owner(): tiles = lax.all_to_all(split_up(shard, dim, size), axis, 0, 0, tiled=True)  19.2 us
    psum x2, blocking collectives, over_axes(): shard = lax.psum(shard, axis)  16 us
    dot_general x1, matrix products, per_device(): jnp.dot(gathered, gate_matrix, preferred_element_type=jnp.float32)  12 us
    reduce_sum x1, other arithmetic, per_device(): weighted = jnp.sum(weights[:, :, None] * selected, axis=1)  8.66 us
  transfers between devices with their start and end apart: 3, of which 2 were waited for; matrix products, arithmetic and copies ran while one was open for 0% of the time, Pallas kernels for 0%

commit v1 on v0

--- a/solution.py
+++ b/solution.py
@@ -67,7 +67,10 @@
     targets, expert_loads = plan_routes(expert_ids, live_counts[0], n_experts, capacity)
     local_slots = targets - my_expert * capacity
     outbound = dispatch_rows(tokens, local_slots, capacity)
-    gathered = lax.all_gather(outbound, DP, axis=0, tiled=True)
+    peers = lax.axis_size(DP)
+    blocks = jnp.stack([outbound for _ in range(peers)])
+    blocks = lax.all_to_all(blocks, DP, split_axis=0, concat_axis=0)
+    gathered = jnp.concatenate(blocks, axis=0)
     gate_matrix = w_gate[0]
     up_matrix = w_up[0]
     down_matrix = w_down[0]

time: 303 us -> 363 us (1.20)
  blocking collectives: 35.2 us -> 184 us
  waiting for transfers between devices: 188 us -> 92.7 us
  local copies, waits for them, and re-layouts: 14.1 us -> 24.8 us
  matrix products: 35.1 us -> 30.8 us
    all_to_all x0 -> x1, blocking collectives: none -> 149 us  [per_device(): blocks = lax.all_to_all(blocks, DP, split_axis=0, concat_axis=0)]
    all_gather x1 -> x0, waiting for transfers between devices: 92.4 us -> none  [per_device(): gathered = lax.all_gather(outbound, DP, axis=0, tiled=True)]
    another operation x1 -> x2, local copies, waits for them, and re-layouts: 0.01 us -> 6.17 us  [the longest x1 6.16 us: per_device(): blocks = jnp.stack([outbound for _ in range(peers)])]
    unnamed x5 -> x11, local copies, waits for them, and re-layouts: 2.55 us -> 7.03 us
  transfers between devices with their start and end apart: 3 -> 2, of which waited for: 2 -> 1; matrix products, arithmetic and copies ran while one was open for 0% -> 0% of each run, Pallas kernels for 0% -> 0%
where the time goes in v1:
time: 363 us
  blocking collectives  184 us (51%)
  waiting for transfers between devices  92.7 us (26%)
  matrix products  30.8 us (8%)
  local copies, waits for them, and re-layouts  24.8 us (7%)
  between operations  14.8 us (4%)
  other arithmetic  10.5 us (3%)
  starting transfers between devices  4.89 us (1%)
    all_to_all x1, blocking collectives, per_device(): blocks = lax.all_to_all(blocks, DP, split_axis=0, concat_axis=0)  149 us
    reduce_scatter x1, waiting for transfers between devices, per_device(): lax.psum_scatter(jnp.dot(hidden, down_matrix, preferred_element_type=jnp....  92.7 us
    dot_general x1, matrix products, per_device(): jnp.dot(hidden, down_matrix, preferred_element_type=jnp.float32)  21.8 us
    all_to_all x1, blocking collectives, sum_at_owner(): tiles = lax.all_to_all(split_up(shard, dim, size), axis, 0, 0, tiled=True)  19.3 us
    psum x2, blocking collectives, over_axes(): shard = lax.psum(shard, axis)  15.9 us
    reduce_sum x1, other arithmetic, per_device(): weighted = jnp.sum(weights[:, :, None] * selected, axis=1)  8.66 us
    dot_general x1, matrix products, per_device(): jnp.dot(gathered, gate_matrix, preferred_element_type=jnp.float32)  8.54 us
  transfers between devices with their start and end apart: 2, of which 1 were waited for; matrix products, arithmetic and copies ran while one was open for 0% of the time, Pallas kernels for 0%

profile of v1, /device:TPU:2, one launch (start us, length us, event | category | flops | bytes accessed | tf_op | source)
XLA Modules:
  0.0 362.8 jit_solution(15301409725315147975)
XLA Ops:
  7.2 0.8 broadcast_multiply_fusion
  8.0 0.8 copy.17
  9.8 0.1 broadcast_in_dim.27
  10.1 0.1 and.20
  10.3 0.6 reduce-window.6
  10.9 0.2 slice_reduce_fusion
  11.5 0.8 copy.20
  12.5 0.4 convolution_convert_fusion.1
  12.9 6.2 %stack.2 = bf16[16,96,4096]{2,1,0:T(8,128)(2,1)} broadcast(bf16[96,4096]{1,0:T(8,128)(2,1)S(1)} %convolution_convert_fusion.1), dimensions={1,2} | broadcast | bytes 13369344 | tf_op jit(solution)/shard_map/stack | solution.py:71
  19.0 149.1 %all_to_all.15 = bf16[16,96,4096]{2,1,0:T(8,128)(2,1)S(1)} all-to-all(bf16[16,96,4096]{2,1,0:T(8,128)(2,1)} %stack.2), channel_id=1, replica_groups=mesh['dp_0'=4,'dp_1'=4,'expert'=8] {'dp_0','dp_1'}, dimensions={0} | all-to-all | bytes 25165824 | tf_op jit(solution)/shard_map/all_to_all | solution.py:72
  168.1 4.5 %copy-done.2 = bf16[16,96,4096]{2,1,0:T(8,128)(2,1)} copy-done((bf16[16,96,4096]{2,1,0:T(8,128)(2,1)}, bf16[16,96,4096]{2,1,0:T(8,128)(2,1)S(1)}, u32[]{:S(2)}) %copy-start.2) | copy-done | bytes 12582936
  172.5 8.5 %fusion.3 = f32[1536,512]{1,0:T(8,128)} fusion(bf16[1536,4096]{1,0:T(8,128)(2,1)S(1)} %bitcast.29, bf16[1,4096,512]{2,1,0:T(8,128)(2,1)S(1)} %copy-done.3), kind=kOutput, calls=%fused_computation.6 | convolution fusion | flops 6442450944 | bytes 19922944 | tf_op jit(solution)/shard_map/dot_general | solution.py:77
  181.1 21.8 %convolution_convert_fusion = bf16[1536,4096]{1,0:T(8,128)(2,1)} fusion(bf16[1,512,4096]{2,1,0:T(8,128)(2,1)} %param.13, bf16[1536,4096]{1,0:T(8,128)(2,1)} %bitcast.30, bf16[1,4096,512]{2,1,0:T(8,128)(2,1)} %param.12, f32[1536,512]{1,0:T(8,128)} %fusion.3), kind=kOutput, calls=%fused_computation.1 | convolution fusion | flops 12895911936 | bytes 36700160 | tf_op jit(solution)/shard_map/dot_general | solution.py:81
  203.1 92.7 %reduce-scatter.2.cloned.1.call-done = bf16[96,4096]{1,0:T(8,128)(2,1)} async-done(((bf16[1536,4096]{1,0:T(8,128)(2,1)}), bf16[96,4096]{1,0:T(8,128)(2,1)}) %reduce-scatter.2.cloned.1.call-update) | async-done | bytes 786448 | tf_op jit(solution)/shard_map/reduce_scatter | solution.py:80
  295.8 5.1 %gather_fusion = bf16[256,4096]{1,0:T(8,128)(2,1)S(1)} fusion(bf16[96,4096]{1,0:T(8,128)(2,1)} %reduce-scatter.2.cloned.1.call-done, s32[1024]{0:T(1024)S(1)} %pad_clamp_fusion), kind=kCustom, calls=%fused_computation | custom fusion | bytes 4195328 | tf_op jit(solution)/shard_map/gather | solution.py:88
  300.9 4.0 %reshape.69 = f32[128,2,4096]{2,1,0:T(2,128)} reshape(bf16[256,4096]{1,0:T(8,128)(2,1)S(1)} %gather_fusion) | data formatting | bytes 6291456 | tf_op jit(solution)/shard_map/convert_element_type | solution.py:88
  304.9 8.7 %multiply_reduce_fusion = bf16[128,4096]{1,0:T(8,128)(2,1)S(1)} fusion(f32[128,2,4096]{2,1,0:T(2,128)} %reshape.69, f32[128,2]{1,0:T(8,128)S(1)} %get-tuple-element.4), kind=kLoop, calls=%fused_computation.8 | loop fusion | flops 1572864 | bytes 5243904 | tf_op jit(solution)/shard_map/reduce_sum | solution.py:90
  313.6 19.3 %all_to_all.16 = bf16[8,16,4096]{2,1,0:T(8,128)(2,1)S(1)} all-to-all(bf16[8,16,4096]{2,1,0:T(8,128)(2,1)S(1)} %bitcast.32), channel_id=1, replica_groups=mesh['dp_0'=4,'dp_1'=4,'expert'=8] {'expert'}, dimensions={0} | all-to-all | bytes 2097152 | tf_op jit(solution)/shard_map/all_to_all | solution.py:17
  332.9 0.1 reduce_sum.44
  333.1 1.1 broadcast_in_dim.31
  334.2 4.9 %all-to-all-start.2 = ((bf16[8,16,4096]{2,1,0:T(8,128)(2,1)}), bf16[8,16,4096]{2,1,0:T(8,128)(2,1)S(1)}, u32[]{:S(2)}, u32[]{:S(2)}) async-start(bf16[8,16,4096]{2,1,0:T(8,128)(2,1)} %broadcast_in_dim.31), calls=%async_computation.3 | async-start | bytes 2097152 | tf_op jit(solution)/shard_map/all_to_all | solution.py:23
  339.0 8.1 %psum.14 = s32[8]{0:T(128)S(1)} all-reduce(s32[8]{0:T(128)S(1)} %get-tuple-element.2), channel_id=1, replica_groups=mesh['dp_0'=4,'dp_1'=4,'expert'=8] {'dp_0'}, use_global_device_ids=true, to_apply=%region_8.9 | all-reduce | flops 8 | bytes 64 | tf_op jit(solution)/shard_map/psum | solution.py:39
  347.1 7.8 %psum.15 = s32[8]{0:T(128)} all-reduce(s32[8]{0:T(128)S(1)} %psum.14), channel_id=1, replica_groups=mesh['dp_0'=4,'dp_1'=4,'expert'=8] {'dp_1'}, use_global_device_ids=true, to_apply=%region_9.10 | all-reduce | flops 8 | bytes 64 | tf_op jit(solution)/shard_map/psum | solution.py:39
  355.0 1.0 copy.25
  (28 shorter events, 1.3 us)
Async XLA Ops:
  7.2 5.3 %copy-start = (bf16[128,4096]{1,0:T(8,128)(2,1)S(1)}, bf16[128,4096]{1,0:T(8,128)(2,1)}, u32[]{:S(2)}) copy-start(bf16[128,4096]{1,0:T(8,128)(2,1)} %param.7) | copy-start | bytes 3145732
  7.2 288.6 %reduce-scatter.2.cloned.1.call-start = ((), (), s32[]{:S(2)}) async-start(), calls=%async_computation.4 | async-start | bytes 13369344 | tf_op jit(solution)/shard_map/reduce_scatter | solution.py:80
  19.0 153.5 %copy-start.3 = (bf16[1,4096,512]{2,1,0:T(8,128)(2,1)S(1)}, bf16[1,4096,512]{2,1,0:T(8,128)(2,1)}, u32[]{:S(2)}) copy-start(bf16[1,4096,512]{2,1,0:T(8,128)(2,1)} %param.11) | copy-start | bytes 12582916
  168.1 4.5 %copy-start.2 = (bf16[16,96,4096]{2,1,0:T(8,128)(2,1)}, bf16[16,96,4096]{2,1,0:T(8,128)(2,1)S(1)}, u32[]{:S(2)}) copy-start(bf16[16,96,4096]{2,1,0:T(8,128)(2,1)S(1)} %all_to_all.15) | copy-start | bytes 37748740
  313.6 42.3 %copy-start.1 = (bf16[128,4096]{1,0:T(8,128)(2,1)S(1)}, bf16[128,4096]{1,0:T(8,128)(2,1)}, u32[]{:S(2)}) copy-start(bf16[128,4096]{1,0:T(8,128)(2,1)} %param.7) | copy-start | bytes 3145732
  334.2 20.8 %all-to-all-start.2 = ((bf16[8,16,4096]{2,1,0:T(8,128)(2,1)}), bf16[8,16,4096]{2,1,0:T(8,128)(2,1)S(1)}, u32[]{:S(2)}, u32[]{:S(2)}) async-start(bf16[8,16,4096]{2,1,0:T(8,128)(2,1)} %broadcast_in_dim.31), calls=%async_computation.3 | async-start | bytes 2097152 | tf_op jit(solution)/shard_map/all_to_all | solution.py:23
Sparse Core Ops, SparseCore 0:
  203.1 92.6 reduce-scatter.1
